TPU v7x, 32 devices: a whole 2x2x4 slice. The times are simulated.
32 devices in a mesh: rep: 16 (over z, y, core), tp: 2 (over x).
Axes of the slice: x: 2, y: 2, z: 4, core: 2. Of those that a mesh axis runs over, the one named last changes fastest.
Arguments:
- activations: bfloat16 [8192, 6144], P('rep', 'tp'), may hold values from -6 to 6
- norm_gain: float32 [6144], replicated, may hold values from 0.5 to 1.5
- query_gain: float32 [128], replicated, may hold values from 0.5 to 18
- key_gain: float32 [128], replicated, may hold values from 0.5 to 18
- project_in: bfloat16 [6144, 24, 384], P('rep', 'tp'), may hold values from -1 to 1
- project_out: bfloat16 [6144, 3072], P('rep', 'tp'), may hold values from -1 to 1
Outputs:
- attended: bfloat16 [8192, 6144], P('rep', 'tp')
- weight_norms: float32 [2], replicated
All inputs are finite; a program needn't handle non-finite values.
Results may differ from a plain program's by a relative error of at most 0.018.
The roundings to bfloat16 on the way count: a program that leaves them out, or rounds other values in their place, can miss the bound.
Values may be sent and summed in bfloat16 or wider, within the bound.
A program may use at most 192 MiB of HBM per device.

v0:
```python
import math
import jax
import jax.numpy as jnp
from jax import lax
from jax.sharding import PartitionSpec as P

D = 6144
HEADS = 24
HEAD_DIM = 128
PATCHES = 256


def layer_norm(values, gain):
    average = jnp.mean(values, -1, keepdims=True)
    centred = values - average
    variance = jnp.mean(centred * centred, -1, keepdims=True)
    return centred * lax.rsqrt(variance + 1e-06) * gain


def shards(activations, norm_gain, query_gain, key_gain, project_in, project_out):
    gathered_rows = lax.all_gather(activations, "tp", axis=1, tiled=True)
    normed = layer_norm(gathered_rows.astype(jnp.float32), norm_gain).astype(jnp.bfloat16)
    tok_rows = normed.shape[0]
    local_heads = project_in.shape[1]
    head_dim = project_in.shape[2] // 3
    piece = lax.all_gather(project_in, "rep", axis=0, tiled=True)
    running = jnp.dot(normed, piece.reshape(piece.shape[0], -1), preferred_element_type=jnp.float32)
    projected = running
    images_here = tok_rows // PATCHES
    projected = projected.reshape(images_here, PATCHES, local_heads, 3 * head_dim)
    queries = layer_norm(projected[..., :head_dim], query_gain).astype(jnp.bfloat16)
    keys_normed = layer_norm(projected[..., head_dim : 2 * head_dim], key_gain).astype(jnp.bfloat16)
    values = projected[..., 2 * head_dim :].astype(jnp.bfloat16)
    scores = jnp.einsum(
        "iphd,iqhd->ihpq", queries, keys_normed, preferred_element_type=jnp.float32
    ) / math.sqrt(head_dim)
    probabilities = jax.nn.softmax(scores, axis=-1).astype(jnp.bfloat16)
    mixed = jnp.einsum("ihpq,iqhd->iphd", probabilities, values, preferred_element_type=jnp.float32)
    mixed = mixed.astype(jnp.bfloat16).reshape(tok_rows, local_heads * head_dim)
    product = lax.dot_general(
        mixed,
        lax.all_gather(project_out, "rep", axis=0, tiled=True),
        (((1,), (1,)), ((), ())),
        preferred_element_type=jnp.float32,
    )
    attended = lax.psum_scatter(product.astype(jnp.bfloat16), "tp", scatter_dimension=1, tiled=True)
    local_in = jnp.sum(jnp.square(project_in.astype(jnp.float32)))
    local_out = jnp.sum(jnp.square(project_out.astype(jnp.float32)))
    total_in, total_out = lax.psum((local_in, local_out), ("rep", "tp"))
    weight_norms = jnp.stack([jnp.sqrt(total_in / (3 * HEADS * HEAD_DIM)), jnp.sqrt(total_out / D)])
    return (attended, weight_norms)


def solution(mesh):
    in_specs = (P("rep", "tp"), P(), P(), P(), P("rep", "tp", None), P("rep", "tp"))
    out_specs = (P("rep", "tp"), P())
    return jax.shard_map(shards, mesh=mesh, in_specs=in_specs, out_specs=out_specs, check_vma=False)
```

profile of v0, /device:TPU:0, one launch (start us, length us, event | category | flops | bytes accessed | tf_op | source)
XLA Modules:
  0.0 571.8 jit_solution(6341764529476445264)
XLA Ops:
  7.2 0.7 all-gather.4.cloned.1.call-update
  7.9 6.0 %copy.10 = bf16[384,12,384]{0,2,1:T(8,128)(2,1)} copy(bf16[384,12,384]{2,0,1:T(8,128)(2,1)} %param.10) | data formatting | bytes 7077888 | tf_op args[4]
  14.1 0.7 all-gather.8.cloned.1.call-update
  14.8 77.8 %all-gather.4.cloned.1.call-done = bf16[512,6144]{1,0:T(8,128)(2,1)} async-done(((bf16[512,3072]{1,0:T(8,128)(2,1)}), bf16[512,6144]{1,0:T(8,128)(2,1)}) %all-gather.4.cloned.1.call-update) | async-done | bytes 6291472 | tf_op jit(solution)/shard_map/all_gather | solution.py:21
  92.6 3.8 convert_reduce_fusion
  96.5 0.7 copy-done
  97.2 1.8 fusion.5
  99.0 6.3 %fusion.7 = bf16[512,6144]{1,0:T(8,128)(2,1)} fusion(bf16[512,6144]{1,0:T(8,128)(2,1)S(1)} %copy-done, f32[6144]{0:T(1024)S(1)} %copy-done.3, f32[512]{0:T(512)S(1)} %add_rsqrt_fusion.2, f32[512]{0:T(512)S(1)} %broadcast_multiply_fusion.2), kind=kLoop, calls=%fused_computation.9 | loop fusion | flops 15728640 | bytes 12611584 | tf_op jit(solution)/shard_map/convert_element_type | solution.py:22
  105.3 265.2 %all-gather.6.cloned.1.call-done = bf16[6144,12,384]{0,2,1:T(8,128)(2,1)} async-done(((bf16[384,12,384]{0,2,1:T(8,128)(2,1)}), bf16[6144,12,384]{0,2,1:T(8,128)(2,1)}) %all-gather.6.cloned.1.call-update) | async-done | bytes 56623120 | tf_op jit(solution)/shard_map/all_gather | solution.py:26
  370.5 37.1 %fusion.1 = f32[2,256,12,384]{3,1,2,0:T(8,128)} fusion(bf16[2,256,6144,1]{2,1,3,0:T(8,128)(2,1)} %bitcast.26, bf16[6144,12,384]{0,2,1:T(8,128)(2,1)} %all-gather.6.cloned.1.call-done), kind=kOutput, calls=%fused_computation.1 | convolution fusion | flops 28991029248 | bytes 72351744 | tf_op jit(solution)/shard_map/dot_general | solution.py:27
  407.6 4.7 slice_reduce_fusion.1
  412.4 5.8 %multiply_reduce_fusion.3 = (f32[2,256,12]{1,2,0:T(8,128)S(1)}, f32[2,256,12]{1,2,0:T(8,128)S(1)}) fusion(f32[2,256,12,384]{3,1,2,0:T(8,128)} %fusion.1, f32[2,256,12]{1,2,0:T(8,128)S(1)} %get-tuple-element.11, f32[2,256,12]{1,2,0:T(8,128)S(1)} %get-tuple-element.10), kind=kLoop, calls=%fused_computation.21 | loop fusion | flops 4706304 | bytes 6389760 | tf_op jit(solution)/shard_map/reduce_sum | solution.py:16
  418.3 3.5 fusion.14
  421.8 5.0 fusion.23
  426.8 0.9 fusion.21
  427.7 1.6 copy.13
  429.7 41.3 %all-gather.8.cloned.1.call-done = bf16[6144,1536]{1,0:T(8,128)(2,1)} async-done(((bf16[384,1536]{1,0:T(8,128)(2,1)}), bf16[6144,1536]{1,0:T(8,128)(2,1)}) %all-gather.8.cloned.1.call-update) | async-done | bytes 18874384 | tf_op jit(solution)/shard_map/all_gather | solution.py:42
  471.0 15.6 %convolution_convert_fusion = bf16[512,6144]{1,0:T(8,128)(2,1)} fusion(bf16[512,1536]{0,1:T(8,128)(2,1)S(1)} %bitcast.28, bf16[6144,1536]{1,0:T(8,128)(2,1)} %all-gather.8.cloned.1.call-done), kind=kOutput, calls=%fused_computation.10 | convolution fusion | flops 9666822144 | bytes 26738688 | tf_op jit(solution)/shard_map/dot_general | solution.py:40
  486.6 2.0 copy-done.2
  488.6 2.4 multiply_reduce_fusion
  491.0 2.5 multiply_reduce_fusion.4
  493.5 41.4 %all-reduce = (f32[]{:T(128)}, f32[]{:T(128)}) all-reduce(f32[]{:T(128)} %multiply_reduce_fusion.4, f32[]{:T(128)} %multiply_reduce_fusion), channel_id=1, replica_groups=mesh['rep'=16,'tp'=2] {'rep','tp'}, use_global_device_ids=true, to_apply=%region_12.0 | all-reduce | flops 2 | bytes 16 | tf_op jit(solution)/shard_map/psum | solution.py:49
  536.2 0.6 pad_maximum_fusion
  536.8 28.5 %reduce-scatter.2.cloned.1.call-done = bf16[512,3072]{1,0:T(8,128)(2,1)} async-done(((bf16[512,6144]{1,0:T(8,128)(2,1)}), bf16[512,3072]{1,0:T(8,128)(2,1)}) %reduce-scatter.2.cloned.1.call-update) | async-done | bytes 3145744 | tf_op jit(solution)/shard_map/reduce_scatter | solution.py:46
  (22 shorter events, 0.6 us)
Async XLA Ops:
  7.2 85.5 %all-gather.4.cloned.1.call-start = ((), (), s32[]{:S(2)}) async-start(), calls=%async_computation.1 | async-start | bytes 9437184 | tf_op jit(solution)/shard_map/all_gather | solution.py:21
  7.9 362.6 %all-gather.6.cloned.1.call-start = ((), (), s32[]{:S(2)}) async-start(), calls=%async_computation.2 | async-start | bytes 60162048 | tf_op jit(solution)/shard_map/all_gather | solution.py:26
  14.0 457.0 %all-gather.8.cloned.1.call-start = ((), (), s32[]{:S(2)}) async-start(), calls=%async_computation.3 | async-start | bytes 20054016 | tf_op jit(solution)/shard_map/all_gather | solution.py:42
  14.1 85.0 %copy-start.3 = (f32[6144]{0:T(1024)S(1)}, f32[6144]{0:T(1024)}, u32[]{:S(2)}) copy-start(f32[6144]{0:T(1024)} %param.7) | copy-start | bytes 73732
  14.7 550.6 %reduce-scatter.2.cloned.1.call-start = ((), (), s32[]{:S(2)}) async-start(), calls=%async_computation.4 | async-start | bytes 9437184 | tf_op jit(solution)/shard_map/reduce_scatter | solution.py:46
  92.6 4.6 copy-start
  407.6 10.6 %copy-start.1 = (f32[2,256,12,384]{3,1,2,0:T(8,128)S(1)}, f32[2,256,12,384]{3,1,2,0:T(8,128)}, u32[]{:S(2)}) copy-start(f32[2,256,12,384]{3,1,2,0:T(8,128)} %fusion.1) | copy-start | bytes 28311556
  407.6 10.6 %copy-start.4 = (f32[128]{0:T(128)S(1)}, f32[128]{0:T(128)}, u32[]{:S(2)}) copy-start(f32[128]{0:T(128)} %param.9) | copy-start | bytes 1540
  407.6 10.6 %copy-start.5 = (f32[128]{0:T(128)S(1)}, f32[128]{0:T(128)}, u32[]{:S(2)}) copy-start(f32[128]{0:T(128)} %param.8) | copy-start | bytes 1540
  486.6 2.0 copy-start.2
Sparse Core Ops, SparseCore 0:
  9.5 83.0 all-gather.3
  94.2 276.2 all-gather.5
  372.1 98.8 all-gather.7
  486.8 78.5 reduce-scatter.1
where the time goes:
time: 572 us
  waiting for transfers between devices  414 us (72%)
  matrix products  57.2 us (10%)
  blocking collectives  41.4 us (7%)
  other arithmetic  33 us (6%)
  between operations  15.2 us (3%)
  local copies, waits for them, and re-layouts  10.7 us (2%)
    all_gather x1, waiting for transfers between devices, shards(): piece = lax.all_gather(project_in, 'rep', axis=0, tiled=True)  265 us
    all_gather x1, waiting for transfers between devices, shards(): gathered_rows = lax.all_gather(activations, 'tp', axis=1, tiled=True)  77.8 us
    psum x1, blocking collectives, shards(): total_in, total_out = lax.psum((local_in, local_out), ('rep', 'tp'))  41.4 us
    all_gather x1, waiting for transfers between devices, shards(): lax.all_gather(project_out, 'rep', axis=0, tiled=True)  41.3 us
    dot_general x1, matrix products, shards(): jnp.dot(normed, piece.reshape(piece.shape[0], -1), preferred_element_type...  37.1 us
    reduce_scatter x1, waiting for transfers between devices, shards(): lax.psum_scatter(product.astype(jnp.bfloat16), 'tp', scatter_dimension=1,...  28.5 us
    dot_general x1, matrix products, shards(): lax.dot_general(mixed, lax.all_gather(project_out, 'rep', axis=0, tiled=T...  15.6 us
  transfers between devices with their start and end apart: 4, of which 4 were waited for; matrix products, arithmetic and copies ran while one was open for 14% of the time, Pallas kernels for 0%

commit v1 on v0

--- a/solution.py
+++ b/solution.py
@@ -10,6 +10,10 @@
 PATCHES = 256
 
 
+def map_the_row(frame_in):
+    return jnp.concatenate(jax.lax.all_gather(frame_in, "tp"), axis=1)
+
+
 def layer_norm(values, gain):
     average = jnp.mean(values, -1, keepdims=True)
     centred = values - average
@@ -18,7 +22,7 @@
 
 
 def shards(activations, norm_gain, query_gain, key_gain, project_in, project_out):
-    gathered_rows = lax.all_gather(activations, "tp", axis=1, tiled=True)
+    gathered_rows = map_the_row(activations)
     normed = layer_norm(gathered_rows.astype(jnp.float32), norm_gain).astype(jnp.bfloat16)
     tok_rows = normed.shape[0]
     local_heads = project_in.shape[1]

time: 572 us -> 573 us (level)
  waiting for transfers between devices: 414 us -> 361 us
  local copies, waits for them, and re-layouts: 10.7 us -> 54 us
  other arithmetic: 33 us -> 43.3 us
    all_gather x1, waiting for transfers between devices: 265 us -> 211 us  [shards(): piece = lax.all_gather(project_in, 'rep', axis=0, tiled=True)]
    mul x0 -> x2, local copies, waits for them, and re-layouts: none -> 29.5 us  [layer_norm(): return centred * lax.rsqrt(variance + 1e-06) * gain]
    convert_element_type x0 -> x1, local copies, waits for them, and re-layouts: none -> 14.5 us  [shards(): layer_norm(gathered_rows.astype(jnp.float32), norm_gain)]
  transfers between devices with their start and end apart: 4 -> 4, of which waited for: 4 -> 4; matrix products, arithmetic and copies ran while one was open for 14% -> 24% of each run, Pallas kernels for 0% -> 0%
where the time goes in v1:
time: 573 us; the launch traced here: 572 us
  waiting for transfers between devices  361 us (63%)
  matrix products  57.1 us (10%)
  local copies, waits for them, and re-layouts  54 us (9%)
  other arithmetic  43.3 us (8%)
  blocking collectives  41.4 us (7%)
  between operations  15.2 us (3%)
    all_gather x1, waiting for transfers between devices, shards(): piece = lax.all_gather(project_in, 'rep', axis=0, tiled=True)  211 us
    all_gather x1, waiting for transfers between devices, map_the_row(): return jnp.concatenate(jax.lax.all_gather(frame_in, 'tp'), axis=1)  77.8 us
    all_gather x1, waiting for transfers between devices, shards(): lax.all_gather(project_out, 'rep', axis=0, tiled=True)  41.4 us
    psum x1, blocking collectives, shards(): total_in, total_out = lax.psum((local_in, local_out), ('rep', 'tp'))  41.4 us
    dot_general x1, matrix products, shards(): jnp.dot(normed, piece.reshape(piece.shape[0], -1), preferred_element_type...  37.1 us
    mul x2, local copies, waits for them, and re-layouts, layer_norm(): return centred * lax.rsqrt(variance + 1e-06) * gain  29.5 us
    reduce_scatter x1, waiting for transfers between devices, shards(): lax.psum_scatter(product.astype(jnp.bfloat16), 'tp', scatter_dimension=1,...  28.5 us
    dot_general x1, matrix products, shards(): lax.dot_general(mixed, lax.all_gather(project_out, 'rep', axis=0, tiled=T...  15.6 us
  transfers between devices with their start and end apart: 4, of which 4 were waited for; matrix products, arithmetic and copies ran while one was open for 24% of the time, Pallas kernels for 0%

profile of v1, /device:TPU:0, one launch (start us, length us, event | category | flops | bytes accessed | tf_op | source)
XLA Modules:
  0.0 571.8 jit_solution(8365091709977114880)
XLA Ops:
  7.2 0.7 all-gather.9.cloned.1.call-update
  8.0 6.0 %copy.17 = bf16[384,12,384]{0,2,1:T(8,128)(2,1)} copy(bf16[384,12,384]{2,0,1:T(8,128)(2,1)} %param.10) | data formatting | bytes 7077888 | tf_op args[4]
  14.8 77.8 %all-gather.9.cloned.1.call-done = bf16[1024,3072]{1,0:T(8,128)(2,1)} async-done(((bf16[512,3072]{1,0:T(8,128)(2,1)}), bf16[1024,3072]{1,0:T(8,128)(2,1)}) %all-gather.9.cloned.1.call-update) | async-done | bytes 6291472 | tf_op jit(solution)/shard_map/all_gather | solution.py:14
  92.6 3.8 convert_reduce_fusion
  96.5 9.9 %convert_element_type.56 = f32[1024,3072]{1,0:T(8,128)} convert(bf16[1024,3072]{1,0:T(8,128)(2,1)} %all-gather.9.cloned.1.call-done) | non-fusion elementwise | flops 3145728 | bytes 18874368 | tf_op jit(solution)/shard_map/convert_element_type | solution.py:26
  106.4 5.9 %multiply_reduce_fusion = f32[512]{0:T(512)S(1)} fusion(f32[2,512,3072]{2,1,0:T(8,128)} %bitcast.29, f32[512]{0:T(512)S(1)} %broadcast_multiply_fusion.2), kind=kLoop, calls=%fused_computation.4 | loop fusion | flops 9436672 | bytes 12587008 | tf_op jit(solution)/shard_map/reduce_sum | solution.py:20
  112.4 2.6 fusion.3
  115.0 29.5 %copy.16 = bf16[512,2,3072]{2,1,0:T(2,128)(2,1)} copy(bf16[512,2,3072]{2,0,1:T(8,128)(2,1)S(1)} %fusion.3) | data formatting | bytes 12582912 | tf_op jit(solution)/shard_map/mul | solution.py:21
  144.5 14.5 %reshape.100 = bf16[2,256,6144,1]{2,1,0,3:T(8,128)(2,1)} reshape(bf16[512,2,3072]{2,1,0:T(2,128)(2,1)} %copy.16) | data formatting | bytes 12582912 | tf_op jit(solution)/shard_map/convert_element_type | solution.py:26
  159.0 211.5 %all-gather.5.cloned.1.call-done = bf16[6144,12,384]{0,2,1:T(8,128)(2,1)} async-done(((bf16[384,12,384]{0,2,1:T(8,128)(2,1)}), bf16[6144,12,384]{0,2,1:T(8,128)(2,1)}) %all-gather.5.cloned.1.call-update) | async-done | bytes 56623120 | tf_op jit(solution)/shard_map/all_gather | solution.py:30
  370.5 37.1 %fusion.1 = f32[2,256,12,384]{3,1,2,0:T(8,128)} fusion(bf16[6144,12,384]{0,2,1:T(8,128)(2,1)} %all-gather.5.cloned.1.call-done, bf16[2,256,6144,1]{2,1,0,3:T(8,128)(2,1)} %reshape.100), kind=kOutput, calls=%fused_computation.1 | convolution fusion | flops 28991029248 | bytes 72351744 | tf_op jit(solution)/shard_map/dot_general | solution.py:31
  407.6 4.7 slice_reduce_fusion.1
  412.4 6.0 %multiply_reduce_fusion.4 = (f32[2,256,12]{1,2,0:T(8,128)S(1)}, f32[2,256,12]{1,2,0:T(8,128)S(1)}) fusion(f32[2,256,12,384]{3,1,2,0:T(8,128)} %fusion.1, f32[2,256,12]{1,2,0:T(8,128)S(1)} %get-tuple-element.11, f32[2,256,12]{1,2,0:T(8,128)S(1)} %get-tuple-element.10), kind=kLoop, calls=%fused_computation.19 | loop fusion | flops 4706304 | bytes 6389760 | tf_op jit(solution)/shard_map/reduce_sum | solution.py:20
  418.4 3.5 fusion.11
  422.0 4.8 fusion.20
  426.8 0.9 fusion.18
  427.6 1.6 copy.20
  429.6 41.4 %all-gather.7.cloned.1.call-done = bf16[6144,1536]{1,0:T(8,128)(2,1)} async-done(((bf16[384,1536]{1,0:T(8,128)(2,1)}), bf16[6144,1536]{1,0:T(8,128)(2,1)}) %all-gather.7.cloned.1.call-update) | async-done | bytes 18874384 | tf_op jit(solution)/shard_map/all_gather | solution.py:46
  471.0 15.6 %convolution_convert_fusion = bf16[512,6144]{1,0:T(8,128)(2,1)} fusion(bf16[512,1536]{0,1:T(8,128)(2,1)S(1)} %bitcast.31, bf16[6144,1536]{1,0:T(8,128)(2,1)} %all-gather.7.cloned.1.call-done), kind=kOutput, calls=%fused_computation.5 | convolution fusion | flops 9666822144 | bytes 26738688 | tf_op jit(solution)/shard_map/dot_general | solution.py:44
  486.6 2.0 copy-done.1
  488.6 2.4 multiply_reduce_fusion.1
  491.0 2.5 multiply_reduce_fusion.5
  493.5 41.4 %all-reduce = (f32[]{:T(128)}, f32[]{:T(128)}) all-reduce(f32[]{:T(128)} %multiply_reduce_fusion.5, f32[]{:T(128)} %multiply_reduce_fusion.1), channel_id=1, replica_groups=mesh['rep'=16,'tp'=2] {'rep','tp'}, use_global_device_ids=true, to_apply=%region_12.0 | all-reduce | flops 2 | bytes 16 | tf_op jit(solution)/shard_map/psum | solution.py:53
  536.8 28.5 %reduce-scatter.2.cloned.1.call-done = bf16[512,3072]{1,0:T(8,128)(2,1)} async-done(((bf16[512,6144]{1,0:T(8,128)(2,1)}), bf16[512,3072]{1,0:T(8,128)(2,1)}) %reduce-scatter.2.cloned.1.call-update) | async-done | bytes 3145744 | tf_op jit(solution)/shard_map/reduce_scatter | solution.py:50
  (31 shorter events, 1.9 us)
Async XLA Ops:
  7.2 85.5 %all-gather.9.cloned.1.call-start = ((), (), s32[]{:S(2)}) async-start(), calls=%async_computation.4 | async-start | bytes 9437184 | tf_op jit(solution)/shard_map/all_gather | solution.py:14
  7.9 6.9 %copy-start.2 = (f32[6144]{0:T(1024)S(1)}, f32[6144]{0:T(1024)}, u32[]{:S(2)}) copy-start(f32[6144]{0:T(1024)} %param.7) | copy-start | bytes 73732
  7.9 362.6 %all-gather.5.cloned.1.call-start = ((), (), s32[]{:S(2)}) async-start(), calls=%async_computation.1 | async-start | bytes 60162048 | tf_op jit(solution)/shard_map/all_gather | solution.py:30
  14.0 457.0 %all-gather.7.cloned.1.call-start = ((), (), s32[]{:S(2)}) async-start(), calls=%async_computation.2 | async-start | bytes 20054016 | tf_op jit(solution)/shard_map/all_gather | solution.py:46
  14.8 550.5 %reduce-scatter.2.cloned.1.call-start = ((), (), s32[]{:S(2)}) async-start(), calls=%async_computation.3 | async-start | bytes 9437184 | tf_op jit(solution)/shard_map/reduce_scatter | solution.py:50
  92.6 19.7 %slice-start = ((s8[6291456]{0:T(1024)(128)(4,1)}), s8[2097152]{0:T(1024)(128)(4,1)S(1)}, s32[]{:S(2)}) async-start(s8[6291456]{0:T(1024)(128)(4,1)} %bitcast.27), calls=%async_computation.5 | async-start | bytes 4194304
  96.5 15.9 %slice-start.1 = ((s8[6291456]{0:T(1024)(128)(4,1)}), s8[4194304]{0:T(1024)(128)(4,1)S(1)}, s32[]{:S(2)}) async-start(s8[6291456]{0:T(1024)(128)(4,1)} %bitcast.27), calls=%async_computation.6 | async-start | bytes 8388608
  407.6 10.8 %copy-start = (f32[2,256,12,384]{3,1,2,0:T(8,128)S(1)}, f32[2,256,12,384]{3,1,2,0:T(8,128)}, u32[]{:S(2)}) copy-start(f32[2,256,12,384]{3,1,2,0:T(8,128)} %fusion.1) | copy-start | bytes 28311556
  407.6 10.8 %copy-start.3 = (f32[128]{0:T(128)S(1)}, f32[128]{0:T(128)}, u32[]{:S(2)}) copy-start(f32[128]{0:T(128)} %param.9) | copy-start | bytes 1540
  407.6 10.8 %copy-start.4 = (f32[128]{0:T(128)S(1)}, f32[128]{0:T(128)}, u32[]{:S(2)}) copy-start(f32[128]{0:T(128)} %param.8) | copy-start | bytes 1540
  486.6 2.0 copy-start.1
Sparse Core Ops, SparseCore 0:
  9.5 83.0 all-gather.8
  94.2 276.2 all-gather.4
  372.1 98.8 all-gather.6
  486.8 78.5 reduce-scatter.1
